TPU v7x, 128 devices: a whole 4x4x4 slice. The times are simulated.
128 devices in a mesh: vec: 4 (over z), row: 32 (over x, y, core).
Axes of the slice: x: 4, y: 4, z: 4, core: 2. Of those that a mesh axis runs over, the one named last changes fastest.
Arguments:
- chol_vectors: float32 [128, 1024, 1024], P('vec', 'row'), may hold values from -16 to 16, as said below
Outputs:
- rotated: float32 [128, 1024, 1024], P('vec', 'row')
- rotation: float32 [1024, 1024], P('row')
Inputs may be any that keep to these rules, and one draw needn't show every extreme that they name: Every matrix chol_vectors[P] is symmetric in its last two dimensions.
All inputs are finite; a program needn't handle non-finite values.
Results may differ from a plain program's by a relative error of at most 0.00014.
Values sent between devices are 32-bit elements; how exact they have to be, the bound alone decides.
A program may use at most 128 MiB of HBM per device.

v0:
```python
import jax
import jax.numpy as jnp
from jax import lax
from jax.sharding import PartitionSpec as P

ITERS = 2


step_gain = 0.2


def from_everyone(x, axis):
    copies = jnp.broadcast_to(x, (lax.axis_size(axis), *x.shape))
    return lax.all_to_all(copies, axis, split_axis=0, concat_axis=0, tiled=True)


def taken_together(x, axis):
    return from_everyone(x, axis).sum(axis=0)


def shards(chol_vectors):
    row_count = chol_vectors.shape[1]
    orbitals = chol_vectors.shape[2]
    offset = lax.axis_index("row") * row_count
    highest = lax.Precision.HIGHEST
    local_rows = lax.broadcasted_iota(jnp.int32, (row_count, orbitals), 0) + offset
    local_cols = lax.broadcasted_iota(jnp.int32, (row_count, orbitals), 1)
    identity_rows = (local_rows == local_cols).astype(jnp.float32)
    current = chol_vectors
    rotation = identity_rows
    for iteration in range(ITERS):
        block = lax.dynamic_slice_in_dim(current, offset, row_count, 2)
        diagonal = jnp.diagonal(block, axis1=1, axis2=2)
        own_part = jnp.einsum("pjk,pj->jk", current, diagonal, precision=highest)
        summed = taken_together(own_part, "vec")
        mirrored = lax.all_to_all(summed, "row", split_axis=1, concat_axis=0, tiled=True)
        gradient = summed - mirrored.T
        squares = taken_together(jnp.sum(gradient * gradient), "row")
        norm = jnp.sqrt(squares / (orbitals * orbitals) + 1e-06)
        generator = step_gain / jnp.sqrt(jnp.float32(orbitals)) * gradient / norm
        generator_full = lax.all_gather(generator, "row", axis=0, tiled=True)
        identity_full = jnp.eye(orbitals, dtype=jnp.float32)
        step_full = (
            identity_full
            + generator_full
            + 0.5 * jnp.dot(generator_full, generator_full, precision=highest)
        )
        step_local = lax.dynamic_slice_in_dim(step_full, offset, row_count, 0)
        if iteration == 0:
            rotation = step_local
        else:
            rotation = jnp.dot(rotation, step_full, precision=highest)
        product_left = jnp.einsum("pjk,kl->pjl", current, step_full, precision=highest)
        columns = lax.all_to_all(product_left, "row", split_axis=2, concat_axis=1, tiled=True)
        current = jnp.einsum("pim,ik->pmk", columns, step_full, precision=highest)
    return (current, rotation)


def solution(mesh):
    placed = (P("vec", "row", None),)
    return jax.shard_map(
        shards,
        mesh=mesh,
        in_specs=placed,
        out_specs=(P("vec", "row", None), P("row", None)),
        check_vma=False,
    )
```

profile of v0, /device:TPU:1, one launch (start us, length us, event | category | flops | bytes accessed | tf_op | source)
XLA Modules:
  0.0 596.7 jit_solution(14842400402261079358)
XLA Ops:
  16.0 14.3 %all_to_all.96 = f32[4,32,1024]{2,1,0:T(8,128)S(1)} all-to-all(f32[4,32,1024]{2,1,0:T(8,128)S(1)} %broadcast_in_dim.18), channel_id=1, replica_groups=mesh['vec'=4,'row'=32] {'vec'}, dimensions={0} | all-to-all | bytes 1048576 | tf_op jit(solution)/shard_map/all_to_all | solution.py:14
  30.8 16.4 %all_to_all.97 = f32[32,1,1024]{2,1,0:T(1,128)S(1)} all-to-all(f32[32,1,1024]{2,1,0:T(1,128)S(1)} %reshape.32), channel_id=1, replica_groups=mesh['vec'=4,'row'=32] {'row'}, dimensions={0} | all-to-all | bytes 262144 | tf_op jit(solution)/shard_map/all_to_all | solution.py:36
  63.4 41.9 %all-gather.3.cloned.1.call-done = f32[1024,1024]{1,0:T(8,128)} async-done(((f32[32,1024]{1,0:T(8,128)}), f32[1024,1024]{1,0:T(8,128)}) %all-gather.3.cloned.1.call-update) | async-done | bytes 4194320 | tf_op jit(solution)/shard_map/all_gather | solution.py:41
  105.3 18.4 %fusion = f32[1024,1024]{1,0:T(8,128)S(1)} fusion(f32[1024,1024]{1,0:T(8,128)} %all-gather.3.cloned.1.call-done), kind=kOutput, calls=%fused_computation.6 | convolution fusion | flops 12890144768 | bytes 8388608 | tf_op jit(solution)/shard_map/dot_general | solution.py:46
  125.7 15.3 %fusion.14 = f32[32,32,1024]{2,1,0:T(8,128)} fusion(f32[32,32,1024]{2,1,0:T(8,128)S(1)} %copy-done, f32[1024,1024]{1,0:T(8,128)S(1)} %fusion), kind=kOutput, calls=%fused_computation.21 | convolution fusion | flops 12884901888 | bytes 12582912 | tf_op jit(solution)/shard_map/pjk,kl->pjl/dot_general | solution.py:53
  141.0 14.4 %copy.33 = f32[32,32,1024]{1,0,2:T(8,128)} copy(f32[32,32,1024]{2,1,0:T(8,128)} %fusion.14) | data formatting | bytes 8388608 | tf_op jit(solution)/shard_map/pjk,kl->pjl/dot_general | solution.py:53
  155.4 16.0 %reshape.34 = f32[32,1,32768]{2,1,0:T(1,128)} reshape(f32[1024,32,32]{2,1,0:T(8,128)} %bitcast.91) | data formatting | bytes 8388608
  171.4 56.3 %all_to_all.99 = f32[32,1,32768]{2,1,0:T(1,128)} all-to-all(f32[32,1,32768]{2,1,0:T(1,128)} %reshape.34), channel_id=1, replica_groups=mesh['vec'=4,'row'=32] {'row'}, dimensions={0} | all-to-all | bytes 8388608 | tf_op jit(solution)/shard_map/all_to_all | solution.py:54
  227.7 13.7 %reduce.3 = f32[32,32768]{1,0:T(8,128)} reduce(f32[32,1,32768]{2,1,0:T(1,128)} %all_to_all.99, f32[]{:T(128)} %broadcast.50), dimensions={1}, to_apply=%all_to_all.74.reduce_sub_computation | reduce | bytes 8388612 | tf_op jit(solution)/shard_map/all_to_all | solution.py:54
  251.2 17.7 %copy.61 = f32[32,32,32,32]{1,2,3,0:T(8,128)} copy(f32[32,32,32,32]{1,0,3,2:T(8,128)} %bitcast.93) | data formatting | bytes 8388608 | tf_op jit(solution)/shard_map/all_to_all | solution.py:54
  268.9 13.7 %all_to_all.77 = f32[32,1024,32]{1,2,0:T(8,128)} reshape(f32[32,32,32,32]{2,1,3,0:T(8,128)} %bitcast.94) | data formatting | bytes 8388608 | tf_op jit(solution)/shard_map/all_to_all | solution.py:54
  282.5 17.3 %fusion.6 = f32[32,32,1024]{2,1,0:T(8,128)S(1)} fusion(f32[32,1024,32]{1,2,0:T(8,128)} %all_to_all.77, f32[1024,1024]{1,0:T(8,128)} %copy-done.4), kind=kOutput, calls=%fused_computation.12 | convolution fusion | flops 12884901888 | bytes 12582912 | tf_op jit(solution)/shard_map/pim,ik->pmk/dot_general | solution.py:55
  309.8 13.1 %all_to_all.100 = f32[4,32,1024]{2,1,0:T(8,128)S(1)} all-to-all(f32[4,32,1024]{2,1,0:T(8,128)S(1)} %broadcast_in_dim.20), channel_id=1, replica_groups=mesh['vec'=4,'row'=32] {'vec'}, dimensions={0} | all-to-all | bytes 1048576 | tf_op jit(solution)/shard_map/all_to_all | solution.py:14
  323.4 12.4 %all_to_all.101 = f32[32,1,1024]{2,1,0:T(1,128)S(1)} all-to-all(f32[32,1,1024]{2,1,0:T(1,128)S(1)} %reshape.36), channel_id=1, replica_groups=mesh['vec'=4,'row'=32] {'row'}, dimensions={0} | all-to-all | bytes 262144 | tf_op jit(solution)/shard_map/all_to_all | solution.py:36
  351.3 42.1 %all-gather.5.cloned.1.call-done = f32[1024,1024]{1,0:T(8,128)} async-done(((f32[32,1024]{1,0:T(8,128)}), f32[1024,1024]{1,0:T(8,128)}) %all-gather.5.cloned.1.call-update) | async-done | bytes 4194320 | tf_op jit(solution)/shard_map/all_gather | solution.py:41
  393.4 18.4 %fusion.1 = f32[1024,1024]{1,0:T(8,128)S(1)} fusion(f32[1024,1024]{1,0:T(8,128)} %all-gather.5.cloned.1.call-done), kind=kOutput, calls=%fused_computation.7 | convolution fusion | flops 12890144768 | bytes 8388608 | tf_op jit(solution)/shard_map/dot_general | solution.py:46
  413.8 14.9 %fusion.4 = f32[32,32,1024]{2,1,0:T(8,128)} fusion(f32[32,32,1024]{2,1,0:T(8,128)S(1)} %copy-done.2, f32[1024,1024]{1,0:T(8,128)S(1)} %fusion.1), kind=kOutput, calls=%fused_computation.10 | convolution fusion | flops 12884901888 | bytes 12582912 | tf_op jit(solution)/shard_map/pjk,kl->pjl/dot_general | solution.py:53
  428.7 14.4 %copy.39 = f32[32,32,1024]{1,0,2:T(8,128)} copy(f32[32,32,1024]{2,1,0:T(8,128)} %fusion.4) | data formatting | bytes 8388608 | tf_op jit(solution)/shard_map/pjk,kl->pjl/dot_general | solution.py:53
  443.0 16.0 %reshape.38 = f32[32,1,32768]{2,1,0:T(1,128)} reshape(f32[1024,32,32]{2,1,0:T(8,128)} %bitcast.92) | data formatting | bytes 8388608
  470.2 46.5 %all-to-all-done.7 = f32[32,1,32768]{2,1,0:T(1,128)} async-done(((f32[32,1,32768]{2,1,0:T(1,128)}), f32[32,1,32768]{2,1,0:T(1,128)}, u32[]{:S(2)}, u32[]{:S(2)}) %all-to-all-start.7) | async-done | bytes 4194336 | tf_op jit(solution)/shard_map/all_to_all | solution.py:54
  516.7 13.7 %reduce.5 = f32[32,32768]{1,0:T(8,128)} reduce(f32[32,1,32768]{2,1,0:T(1,128)} %all-to-all-done.7, f32[]{:T(128)} %broadcast.50), dimensions={1}, to_apply=%all_to_all.84.reduce_sub_computation | reduce | bytes 8388612 | tf_op jit(solution)/shard_map/all_to_all | solution.py:54
  540.2 17.7 %copy.60 = f32[32,32,32,32]{1,2,3,0:T(8,128)} copy(f32[32,32,32,32]{1,0,3,2:T(8,128)} %bitcast.95) | data formatting | bytes 8388608 | tf_op jit(solution)/shard_map/all_to_all | solution.py:54
  557.9 13.7 %all_to_all.87 = f32[32,1024,32]{1,2,0:T(8,128)} reshape(f32[32,32,32,32]{2,1,3,0:T(8,128)} %bitcast.96) | data formatting | bytes 8388608 | tf_op jit(solution)/shard_map/all_to_all | solution.py:54
  571.6 17.8 %fusion.2 = f32[32,32,1024]{2,1,0:T(8,128)} fusion(f32[32,1024,32]{1,2,0:T(8,128)} %all_to_all.87, f32[1024,1024]{1,0:T(8,128)} %copy-done.3), kind=kOutput, calls=%fused_computation.8 | convolution fusion | flops 12884901888 | bytes 12582912 | tf_op jit(solution)/shard_map/pim,ik->pmk/dot_general | solution.py:55
  (58 shorter events, 84.8 us)
Async XLA Ops:
  7.2 98.1 %all-gather.3.cloned.1.call-start = ((), (), s32[]{:S(2)}) async-start(), calls=%async_computation.8 | async-start | bytes 4325376 | tf_op jit(solution)/shard_map/all_gather | solution.py:41
  63.2 330.3 %all-gather.5.cloned.1.call-start = ((), (), s32[]{:S(2)}) async-start(), calls=%async_computation.9 | async-start | bytes 4325376 | tf_op jit(solution)/shard_map/all_gather | solution.py:41
  105.3 20.5 %copy-start = (f32[32,32,1024]{2,1,0:T(8,128)S(1)}, f32[32,32,1024]{2,1,0:T(8,128)}, u32[]{:S(2)}) copy-start(f32[32,32,1024]{2,1,0:T(8,128)} %param.1) | copy-start | bytes 12582916
  123.7 2.0 copy-start.4
  299.9 2.0 copy-start.1
  393.4 20.4 %copy-start.2 = (f32[32,32,1024]{2,1,0:T(8,128)S(1)}, f32[32,32,1024]{2,1,0:T(8,128)}, u32[]{:S(2)}) copy-start(f32[32,32,1024]{2,1,0:T(8,128)} %copy-done.1) | copy-start | bytes 12582916
  411.8 1.9 copy-start.3
  459.0 57.7 %all-to-all-start.7 = ((f32[32,1,32768]{2,1,0:T(1,128)}), f32[32,1,32768]{2,1,0:T(1,128)}, u32[]{:S(2)}, u32[]{:S(2)}) async-start(f32[32,1,32768]{2,1,0:T(1,128)} %reshape.38), calls=%async_computation.7 | async-start | bytes 8388608 | tf_op jit(solution)/shard_map/all_to_all | solution.py:54
Sparse Core Ops, SparseCore 0:
  63.3 41.9 all-gather.2
  351.4 41.9 all-gather.4
where the time goes:
time: 605 us; the launch traced here: 597 us
  local copies, waits for them, and re-layouts  157 us (26%)
  blocking collectives  134 us (22%)
  waiting for transfers between devices  131 us (22%)
  matrix products  121 us (20%)
  other arithmetic  33 us (5%)
  between operations  16.2 us (3%)
  starting transfers between devices  6.05 us (1%)
    all_gather x2, waiting for transfers between devices, shards(): generator_full = lax.all_gather(generator, 'row', axis=0, tiled=True)  84 us
    all_to_all x4, local copies, waits for them, and re-layouts, shards(): lax.all_to_all(product_left, 'row', split_axis=2, concat_axis=1, tiled=True)  62.7 us
    unnamed x19, local copies, waits for them, and re-layouts  58.8 us
    all_to_all x1, blocking collectives, shards(): lax.all_to_all(product_left, 'row', split_axis=2, concat_axis=1, tiled=True)  56.3 us
    all_to_all x4, blocking collectives, from_everyone(): return lax.all_to_all(copies, axis, split_axis=0, concat_axis=0, tiled=True)  48.5 us
    all_to_all x1, waiting for transfers between devices, shards(): lax.all_to_all(product_left, 'row', split_axis=2, concat_axis=1, tiled=True)  46.5 us
    dot_general x2, matrix products, shards(): jnp.dot(generator_full, generator_full, precision=highest)  36.8 us
    dot_general x2, matrix products, shards(): current = jnp.einsum('pim,ik->pmk', columns, step_full, precision=highest)  35.1 us
  transfers between devices with their start and end apart: 3, of which 3 were waited for; matrix products, arithmetic and copies ran while one was open for 1% of the time, Pallas kernels for 0%

commit v1 on v0

v1 whole, which is shorter than its diff:
```python
import functools

import jax
import jax.numpy as jnp
from jax import lax
from jax.experimental import pallas as pl
from jax.experimental.pallas import tpu as pltpu
from jax.sharding import PartitionSpec as P

N = 1024
NV = 4
NR = 32
VECS = 32
ROWS = 32
GROUPS = 4
GW = N // GROUPS
GP = VECS // GROUPS
STEP_GAIN = 0.2
PARTS = ((0, 384, "zyx"), (384, 384, "xzy"), (768, 256, "yxz"))
MESH = pl.DeviceIdType.MESH
F32 = jnp.float32
BF16 = jnp.bfloat16


def split(x):
    high = x.astype(BF16)
    return high, (x - high.astype(F32)).astype(BF16)


def dot3(ah, al, bh, bl):
    dot = functools.partial(jnp.dot, preferred_element_type=F32)
    return dot(ah, bh) + dot(ah, bl) + dot(al, bh)


def kernel(
    x_ref, out_ref, rot_ref,
    xf, dbuf, own, zin, full1, full2, gf, s1h, s1l, s2h, s2l, s2th, s2tl,
    l1, l1th, l1tl, dpart, din, dfull, zbuf, ah, al, stage, rh, rl,
    x_sem, zs_s, zs_r, ag_s, ag_r, co_s, co_r, d_s, d_r, db_s, db_r, big_s, big_r, out_sem,
):
    v = lax.axis_index("vec")
    r = lax.axis_index("row")
    cx, cy, cc = r // 8, (r // 2) % 4, r % 2

    load = pltpu.make_async_copy(x_ref, xf, x_sem)
    load.start()
    barrier = pltpu.get_barrier_semaphore()

    @pl.loop(1, NR)
    def _(k):
        pl.semaphore_signal(barrier, inc=1, device_id=(v, (r + k) % NR), device_id_type=MESH)

    @pl.loop(1, NV)
    def _(k):
        pl.semaphore_signal(barrier, inc=1, device_id=((v + k) % NV, r), device_id_type=MESH)

    load.wait()

    window = pl.multiple_of((r // 4) * 128, 128)
    lane = lax.broadcasted_iota(jnp.int32, (8, ROWS, 128), 2)
    sub = lax.broadcasted_iota(jnp.int32, (8, ROWS, 128), 1)

    @pl.loop(0, VECS // 8)
    def _(g):
        block = xf[pl.ds(g * 8, 8), :, pl.ds(window, 128)]
        picked = jnp.where(lane == sub + (r % 4) * ROWS, block, 0.0)
        dbuf[pl.ds(g * 8, 8)] = jnp.broadcast_to(
            jnp.sum(picked, axis=2, keepdims=True), (8, ROWS, 128)
        )

    def weighted(source, weight_of):
        for t in range(0, N, 256):
            def body(p, acc):
                return acc + source(p, t) * weight_of(p, t)
            acc = lax.fori_loop(0, VECS, body, jnp.zeros((ROWS, 256), F32), unroll=4)
            own[:, :, pl.ds(t, 256)] = acc.reshape(NV, 8, 256)

    def wide(d):
        return jnp.concatenate([d, d], axis=1)

    weighted(lambda p, t: xf[p, :, pl.ds(t, 256)], lambda p, t: wide(dbuf[p]))
    pl.semaphore_wait(barrier, NR - 1 + NV - 1)

    def exchange(full, which, filler):
        full6 = full.reshape(4, 4, 2, 4, 8, N)

        def zcopy(k):
            to = (v + k) % NV
            return pltpu.make_async_remote_copy(
                src_ref=own.at[to], dst_ref=zin.at[which, k - 1],
                send_sem=zs_s.at[which, k - 1], recv_sem=zs_r.at[which, k - 1],
                device_id=(to, r), device_id_type=MESH)

        zcopies = [zcopy(k) for k in range(1, NV)]
        for c in zcopies:
            c.start()
        for c in zcopies:
            c.wait()
        piece = own[v] + zin[which, 0] + zin[which, 1] + zin[which, 2]
        full6[cx, cy, cc, v] = piece

        def region(part, have, at):
            lo, n, _ = PARTS[part]
            ix, iy, iz = (
                pl.ds(0, 4) if d in have else pl.ds(at[d], 1) for d in "xyz")
            return full6.at[ix, iy, pl.ds(at["c"], 1), iz, :, pl.ds(lo, n)]

        me = dict(x=cx, y=cy, z=v, c=cc)

        def peer(d, k):
            at = dict(me)
            at[d] = (me[d] + k) % 4
            return at

        def device(at):
            return (at["z"], at["x"] * 8 + at["y"] * 2 + at["c"])

        def ag(part, phase, k):
            order = PARTS[part][2]
            have = order[:phase]
            return pltpu.make_async_remote_copy(
                src_ref=region(part, have, me), dst_ref=region(part, have, me),
                send_sem=ag_s.at[which, part, phase, k - 1],
                recv_sem=ag_r.at[which, part, phase, k - 1],
                device_id=device(peer(order[phase], k)), device_id_type=MESH)

        def ag_in(part, phase, k):
            order = PARTS[part][2]
            have = order[:phase]
            at = peer(order[phase], 4 - k)
            return at, pltpu.make_async_remote_copy(
                src_ref=region(part, have, at), dst_ref=region(part, have, at),
                send_sem=ag_s.at[which, part, phase, k - 1],
                recv_sem=ag_r.at[which, part, phase, k - 1],
                device_id=device(at), device_id_type=MESH)

        def core(part, phase, k, at):
            have = PARTS[part][2][:phase]
            return pltpu.make_async_remote_copy(
                src_ref=region(part, have, at), dst_ref=region(part, have, at),
                send_sem=co_s.at[which, part, phase, k],
                recv_sem=co_r.at[which, part, phase, k],
                device_id=device(dict(me, c=1 - cc)), device_id_type=MESH)

        sends = []
        for phase in range(4):
            for part in range(3):
                if phase:
                    for k in (1, 3, 2):
                        at, incoming = ag_in(part, phase - 1, k)
                        incoming.wait_recv()
                        c = core(part, phase - 1, k, at)
                        c.start()
                        sends.append((c, part, phase - 1, k, at))
                if phase < 3:
                    for k in (2, 1, 3):
                        c = ag(part, phase, k)
                        c.start()
                        sends.append((c,))
                if phase == 0:
                    c = core(part, 0, 0, me)
                    c.start()
                    sends.append((c, part, 0, 0, me))
            if phase < 3:
                filler(phase)
        for s in sends:
            if len(s) > 1:
                _, part, phase, k, at = s
                core(part, phase, k, dict(at, c=1 - cc)).wait_recv()
        for s in sends:
            s[0].wait_send()

    def nothing(phase):
        pass

    exchange(full1, 0, nothing)

    def antisymmetric(full, high, low):
        def body(i, acc):
            at = pl.multiple_of(i * 128, 128)
            strip = full[pl.ds(at, 128), :] - full[:, pl.ds(at, 128)].T
            gf[pl.ds(at, 128), :] = strip
            h, l = split(strip)
            high[pl.ds(at, 128), :] = h
            low[pl.ds(at, 128), :] = l
            square = strip * strip
            return acc + jnp.sum(square.reshape(16, 8, N), axis=0)
        acc = lax.fori_loop(0, N // 128, body, jnp.zeros((8, N), F32))
        total = jnp.sum(jnp.sum(acc, axis=1, keepdims=True), axis=0, keepdims=True)
        norm = jnp.sqrt(total / (N * N) + 1e-06)
        return (STEP_GAIN / (N ** 0.5)) / norm

    def tiles(m, n, body):
        @pl.loop(0, (N // m) * (N // n))
        def _(t):
            i = pl.multiple_of((t // (N // n)) * m, m)
            j = pl.multiple_of((t % (N // n)) * n, n)
            body(i, j)

    def eye(i, j, m, n):
        rows = lax.broadcasted_iota(jnp.int32, (m, n), 0) + i
        cols = lax.broadcasted_iota(jnp.int32, (m, n), 1) + j
        return (rows == cols).astype(F32)

    scale = antisymmetric(full1, ah, al)

    def step1(i, j):
        rows, cols = pl.ds(i, 256), pl.ds(j, 256)
        sq = dot3(ah[rows, :], al[rows, :], ah[:, cols], al[:, cols])
        s = eye(i, j, 256, 256) + scale * gf[rows, cols] + (0.5 * scale * scale) * sq
        h, l = split(s)
        s1h[rows, cols] = h
        s1l[rows, cols] = l

    tiles(256, 256, step1)

    def left(i, j):
        rows, cols = pl.ds(i, 256), pl.ds(j, 256)
        xh, xl = split(xf[pl.ds(i // ROWS, 8), :, :].reshape(256, N))
        l1[pl.ds(i // ROWS, 8), :, cols] = dot3(xh, xl, s1h[:, cols], s1l[:, cols]).reshape(8, ROWS, 256)

    tiles(256, 256, left)

    mine = pl.ds(pl.multiple_of(r * ROWS, ROWS), ROWS)
    for t in range(8):
        cols = pl.ds(t * 128, 128)
        weight = s1h[mine, cols].astype(F32) + s1l[mine, cols].astype(F32)

        @pl.loop(0, VECS, unroll=4)
        def _(p):
            dpart[p, pl.ds(t, 1), :] = jnp.sum(l1[p, :, cols] * weight, axis=0, keepdims=True)

    def dsend(k):
        to = (r + k) % NR
        return pltpu.make_async_remote_copy(
            src_ref=dpart.at[to], dst_ref=din.at[k], send_sem=d_s.at[k], recv_sem=d_r.at[k],
            device_id=(v, to), device_id_type=MESH)

    def dback(k):
        to = (r + k) % NR
        return pltpu.make_async_remote_copy(
            src_ref=din.at[0], dst_ref=dfull.at[r], send_sem=db_s.at[k], recv_sem=db_r.at[k],
            device_id=(v, to), device_id_type=MESH)

    def dback_in(k):
        source = (r + NR - k) % NR
        return pltpu.make_async_remote_copy(
            src_ref=din.at[0], dst_ref=dfull.at[source], send_sem=db_s.at[k], recv_sem=db_r.at[k],
            device_id=(v, source), device_id_type=MESH)

    @pl.loop(1, NR)
    def _(k):
        dsend(k).start()

    @pl.loop(1, NR)
    def _(k):
        dsend(k).wait_recv()

    total = dpart[r] + jnp.sum(din[pl.ds(1, NR - 1)], axis=0)
    din[0] = total
    dfull[r] = total

    @pl.loop(1, NR)
    def _(k):
        dback(k).start()

    def transposed(i):
        at = pl.multiple_of(i * 128, 128)
        strip = l1[pl.ds(i * 4, 4), :, :].reshape(128, N).T
        h, l = split(strip)
        l1th[:, pl.ds(at, 128)] = h
        l1tl[:, pl.ds(at, 128)] = l

    @pl.loop(0, N // 128)
    def _(i):
        transposed(i)

    @pl.loop(1, NR)
    def _(k):
        dback_in(k).wait_recv()

    @pl.loop(1, NR)
    def _(k):
        dsend(k).wait_send()
        dback(k).wait_send()

    for t in range(8):
        cols = pl.ds(t * 128, 128)
        def body(p, acc):
            return acc + l1[p, :, cols] * dfull[p, pl.ds(t, 1), :]
        acc = lax.fori_loop(0, VECS, body, jnp.zeros((ROWS, 128), F32), unroll=4)
        own[:, :, cols] = acc.reshape(NV, 8, 128)

    exchange(full2, 1, nothing)

    @pl.loop(0, N // 128)
    def _(i):
        at = pl.multiple_of(i * 128, 128)
        h, l = split(full2[pl.ds(at, 128), :].T)
        ah[:, pl.ds(at, 128)] = h
        al[:, pl.ds(at, 128)] = l

    def own2(i, j):
        rows, cols = pl.ds(i, 256), pl.ds(j, 256)
        gtmp[rows, cols] = dot3(ah[rows, :], al[rows, :], s1h[:, cols], s1l[:, cols])

    gtmp = stage
    tiles(256, 256, own2)
    scale2 = antisymmetric(gtmp, ah, al)

    def step2(i, j):
        rows, cols = pl.ds(i, 256), pl.ds(j, 256)
        sq = dot3(ah[rows, :], al[rows, :], ah[:, cols], al[:, cols])
        even = eye(i, j, 256, 256) + (0.5 * scale2 * scale2) * sq
        odd = scale2 * gf[rows, cols]
        h, l = split(even + odd)
        s2h[rows, cols] = h
        s2l[rows, cols] = l
        h, l = split(even - odd)
        s2th[rows, cols] = h
        s2tl[rows, cols] = l

    tiles(256, 256, step2)

    def big(g, k):
        to = (r + k) % NR
        lanes = pl.ds(g * GW, GW)
        return pltpu.make_async_remote_copy(
            src_ref=stage.at[pl.ds(pl.multiple_of(to * ROWS, ROWS), ROWS), lanes],
            dst_ref=zbuf.at[mine, lanes],
            send_sem=big_s.at[g, k], recv_sem=big_r.at[g, k],
            device_id=(v, to), device_id_type=MESH)

    def big_in(g, k):
        source = (r + NR - k) % NR
        lanes = pl.ds(g * GW, GW)
        return pltpu.make_async_remote_copy(
            src_ref=stage.at[mine, lanes],
            dst_ref=zbuf.at[pl.ds(pl.multiple_of(source * ROWS, ROWS), ROWS), lanes],
            send_sem=big_s.at[g, k], recv_sem=big_r.at[g, k],
            device_id=(v, source), device_id_type=MESH)

    for g in range(GROUPS):
        lanes = pl.ds(g * GW, GW)

        @pl.loop(0, 4)
        def _(i):
            rows = pl.ds(pl.multiple_of(i * 256, 256), 256)
            stage[rows, lanes] = dot3(s2th[rows, :], s2tl[rows, :], l1th[:, lanes], l1tl[:, lanes])

        zbuf[mine, lanes] = stage[mine, lanes]

        @pl.loop(1, NR)
        def _(k):
            big(g, k).start()

    def rotation(i, j):
        rows, cols = pl.ds(i, 256), pl.ds(j, 256)
        h, l = split(dot3(s1h[rows, :], s1l[rows, :], s2h[:, cols], s2l[:, cols]))
        rh[rows, cols] = h
        rl[rows, cols] = l

    tiles(256, 256, rotation)
    rot_ref[...] = rh[mine, :].astype(F32) + rl[mine, :].astype(F32)

    group = lax.broadcasted_iota(jnp.int32, (ROWS, 128), 1) // ROWS

    def put(g):
        return pltpu.make_async_copy(xf.at[pl.ds(g * GP, GP)], out_ref.at[pl.ds(g * GP, GP)], out_sem.at[g])

    for g in range(GROUPS):
        @pl.loop(1, NR)
        def _(k):
            big_in(g, k).wait_recv()

        @pl.loop(0, 8)
        def _(b4):
            for q in range(GW // 128):
                blocks = [
                    zbuf[pl.ds(pl.multiple_of(b4 * 128 + b * ROWS, ROWS), ROWS), pl.ds(g * GW + q * 128, 128)]
                    for b in range(4)]
                for p in range(4):
                    out = blocks[p]
                    for b in range(4):
                        if b != p:
                            turned = pltpu.roll(blocks[b], (ROWS * (b - p)) % 128, 1)
                            out = jnp.where(group == b, turned, out)
                    h, l = split(out)
                    rows = pl.ds((q * 4 + p) * ROWS, ROWS)
                    cols = pl.ds(pl.multiple_of(b4 * 128, 128), 128)
                    ah[rows, cols] = h
                    al[rows, cols] = l

        @pl.loop(0, 4)
        def _(j):
            cols = pl.ds(pl.multiple_of(j * 256, 256), 256)
            res = dot3(ah[pl.ds(0, GW), :], al[pl.ds(0, GW), :], rh[:, cols], rl[:, cols])
            xf[pl.ds(g * GP, GP), :, cols] = res.reshape(GP, ROWS, 256)

        put(g).start()

    for g in range(GROUPS):
        put(g).wait()

        @pl.loop(1, NR)
        def _(k):
            big(g, k).wait_send()


def shards(chol_vectors):
    full = pltpu.VMEM((N, N), F32)
    half = pltpu.VMEM((N, N), BF16)
    sem = pltpu.SemaphoreType.DMA
    return pl.pallas_call(
        kernel,
        out_shape=(
            jax.ShapeDtypeStruct((VECS, ROWS, N), F32),
            jax.ShapeDtypeStruct((ROWS, N), F32),
        ),
        in_specs=[pl.BlockSpec(memory_space=pl.ANY)],
        out_specs=(pl.BlockSpec(memory_space=pl.ANY), pl.BlockSpec(memory_space=pltpu.VMEM)),
        scratch_shapes=[
            pltpu.VMEM((VECS, ROWS, N), F32),
            pltpu.VMEM((VECS, ROWS, 128), F32),
            pltpu.VMEM((NV, 8, N), F32),
            pltpu.VMEM((2, NV - 1, 8, N), F32),
            full,
            full,
            full,
            half, half, half, half, half, half,
            pltpu.VMEM((VECS, ROWS, N), F32),
            half, half,
            pltpu.VMEM((VECS, 8, 128), F32),
            pltpu.VMEM((NR, 8, 128), F32),
            pltpu.VMEM((NR, 8, 128), F32),
            full,
            half, half,
            full,
            half, half,
            sem,
            sem((2, 3)), sem((2, 3)),
            sem((2, 3, 3, 3)), sem((2, 3, 3, 3)),
            sem((2, 3, 3, 4)), sem((2, 3, 3, 4)),
            sem((NR,)), sem((NR,)), sem((NR,)), sem((NR,)),
            sem((GROUPS, NR)), sem((GROUPS, NR)),
            sem((GROUPS,)),
        ],
        compiler_params=pltpu.CompilerParams(
            collective_id=0, has_side_effects=True, vmem_limit_bytes=67043328
        ),
    )(chol_vectors)


def solution(mesh):
    return jax.shard_map(
        shards,
        mesh=mesh,
        in_specs=(P("vec", "row", None),),
        out_specs=(P("vec", "row", None), P("row", None)),
        check_vma=False,
    )
```

time: 605 us -> 193 us (0.32)
  Pallas kernels: 0 us -> 184 us
  local copies, waits for them, and re-layouts: 157 us -> 5.48 us
  blocking collectives: 134 us -> 0 us
  waiting for transfers between devices: 131 us -> 0 us
  matrix products: 121 us -> 0 us
  other arithmetic: 33 us -> 0 us
  between operations: 16.2 us -> 0.65 us
  starting transfers between devices: 6.05 us -> 0 us
    pallas_call x0 -> x1, Pallas kernels: none -> 184 us  [shards(): pl.pallas_call(kernel, out_shape=(jax.ShapeDtypeStruct((VECS, ROWS, N), F...]
    all_to_all x7 -> x0, blocking collectives: 134 us -> none  [the longest x1 56.3 us: shards(): lax.all_to_all(product_left, 'row', split_axis=2, concat_axis=1, tiled=True)]
    dot_general x9 -> x0, matrix products: 121 us -> none  [the longest x2 36.8 us: shards(): jnp.dot(generator_full, generator_full, precision=highest)]
    all_gather x2 -> x0, waiting for transfers between devices: 84 us -> none  [shards(): generator_full = lax.all_gather(generator, 'row', axis=0, tiled=True)]
    all_to_all x13 -> x0, local copies, waits for them, and re-layouts: 64.8 us -> none  [the longest x4 62.7 us: shards(): lax.all_to_all(product_left, 'row', split_axis=2, concat_axis=1, tiled=True)]
    unnamed x19 -> x4, local copies, waits for them, and re-layouts: 58.8 us -> 5.48 us
    all_to_all x1 -> x0, waiting for transfers between devices: 46.5 us -> none  [shards(): lax.all_to_all(product_left, 'row', split_axis=2, concat_axis=1, tiled=True)]
    all_to_all x4 -> x0, other arithmetic: 29 us -> none  [the longest x2 27.3 us: shards(): lax.all_to_all(product_left, 'row', split_axis=2, concat_axis=1, tiled=True)]
  transfers between devices with their start and end apart: 3 -> 0, of which waited for: 3 -> 0; matrix products, arithmetic and copies ran while one was open for 1% -> 0% of each run, Pallas kernels for 0% -> 0%
where the time goes in v1:
time: 193 us; the launch traced here: 190 us
  Pallas kernels  184 us (95%)
  local copies, waits for them, and re-layouts  5.48 us (3%)
    pallas_call x1, Pallas kernels, shards(): pl.pallas_call(kernel, out_shape=(jax.ShapeDtypeStruct((VECS, ROWS, N), F...  184 us
    unnamed x4, local copies, waits for them, and re-layouts  5.48 us

profile of v1, /device:TPU:1, one launch (start us, length us, event | category | flops | bytes accessed | tf_op | source)
XLA Modules:
  0.0 189.7 jit_solution(2372248641144196000)
XLA Ops:
  0.6 183.5 %shard_map.30 = (f32[32,32,1024]{2,1,0:T(8,128)}, f32[32,1024]{1,0:T(8,128)}) custom-call(f32[32,32,1024]{2,1,0:T(8,128)} %x_ref.1), custom_call_target="tpu_custom_call" | custom-call | tf_op jit(solution)/shard_map/pallas_call | solution.py:414
  184.2 0.0 copy-start
  184.2 4.8 %copy.5 = f32[32,32,1024]{2,1,0:T(8,128)} copy(f32[32,32,1024]{2,1,0:T(8,128)} %get-tuple-element.4) | data formatting | bytes 8388608
  189.0 0.0 copy-done
  189.0 0.7 copy.6
Async XLA Ops:
  184.2 4.8 %copy-start = (f32[32,1024]{1,0:T(8,128)S(1)}, f32[32,1024]{1,0:T(8,128)}, u32[]{:S(2)}) copy-start(f32[32,1024]{1,0:T(8,128)} %get-tuple-element.5) | copy-start | bytes 393220

commit v2 on v1

v2 whole, which is shorter than its diff:
```python
import functools

import jax
import jax.numpy as jnp
from jax import lax
from jax.experimental import pallas as pl
from jax.experimental.pallas import tpu as pltpu
from jax.sharding import PartitionSpec as P

N = 1024
NV = 4
NR = 32
VECS = 32
ROWS = 32
GROUPS = 4
GW = N // GROUPS
GP = VECS // GROUPS
STEP_GAIN = 0.2
VMEM_LIMIT = 58 << 20
PARTS = ((0, 384, "zyx"), (384, 384, "xzy"), (768, 256, "yxz"))
OFFSETS = tuple(sorted(
    ((dx, dy, dc) for dx in range(4) for dy in range(4) for dc in range(2) if dx or dy or dc),
    key=lambda o: -(min(o[0], 4 - o[0]) + min(o[1], 4 - o[1]))))
MESH = pl.DeviceIdType.MESH
F32 = jnp.float32
BF16 = jnp.bfloat16


def split(x):
    high = x.astype(BF16)
    return high, (x - high.astype(F32)).astype(BF16)


def dot3(ah, al, bh, bl):
    dot = functools.partial(jnp.dot, preferred_element_type=F32)
    return dot(ah, bh) + dot(ah, bl) + dot(al, bh)


def kernel(
    x_ref, out_ref, rot_ref,
    xf, dbuf, own, zin, full1, full2, gf, s1h, s1l, s2h, s2l,
    l1, l1th, l1tl, dpart, din, dfull, zbuf, ah, al, stage, rh, rl, wh, wl, lh, ll,
    x_sem, zs_s, zs_r, ag_s, ag_r, co_s, co_r, d_sem, big_s, big_r,
):
    v = lax.axis_index("vec")
    r = lax.axis_index("row")
    cx, cy, cc = r // 8, (r // 2) % 4, r % 2

    load = pltpu.make_async_copy(x_ref, xf, x_sem)
    load.start()
    barrier = pltpu.get_barrier_semaphore()

    @pl.loop(1, NR)
    def _(k):
        pl.semaphore_signal(barrier, inc=1, device_id=(v, (r + k) % NR), device_id_type=MESH)

    @pl.loop(1, NV)
    def _(k):
        pl.semaphore_signal(barrier, inc=1, device_id=((v + k) % NV, r), device_id_type=MESH)

    load.wait()

    window = pl.multiple_of((r // 4) * 128, 128)
    lane = lax.broadcasted_iota(jnp.int32, (8, ROWS, 128), 2)
    sub = lax.broadcasted_iota(jnp.int32, (8, ROWS, 128), 1)

    @pl.loop(0, VECS // 8)
    def _(g):
        block = xf[pl.ds(g * 8, 8), :, pl.ds(window, 128)]
        picked = jnp.where(lane == sub + (r % 4) * ROWS, block, 0.0)
        dbuf[pl.ds(g * 8, 8)] = jnp.broadcast_to(
            jnp.sum(picked, axis=2, keepdims=True), (8, ROWS, 128)
        )

    def weighted(source, weight_of):
        for t in range(0, N, 256):
            def body(p, acc):
                return acc + source(p, t) * weight_of(p, t)
            acc = lax.fori_loop(0, VECS, body, jnp.zeros((ROWS, 256), F32), unroll=4)
            own[:, :, pl.ds(t, 256)] = acc.reshape(NV, 8, 256)

    def wide(d):
        return jnp.concatenate([d, d], axis=1)

    weighted(lambda p, t: xf[p, :, pl.ds(t, 256)], lambda p, t: wide(dbuf[p]))
    pl.semaphore_wait(barrier, NR - 1 + NV - 1)

    def exchange(full, which, filler):
        full6 = full.reshape(4, 4, 2, 4, 8, N)

        def zcopy(k):
            to = (v + k) % NV
            return pltpu.make_async_remote_copy(
                src_ref=own.at[to], dst_ref=zin.at[which, k - 1],
                send_sem=zs_s.at[which], recv_sem=zs_r.at[which],
                device_id=(to, r), device_id_type=MESH)

        zcopies = [zcopy(k) for k in range(1, NV)]
        for c in zcopies:
            c.start()
        def taken(ref, sem):
            pltpu.make_async_copy(ref, ref, sem).wait()

        taken(zin.at[which], zs_r.at[which])
        piece = own[v] + zin[which, 0] + zin[which, 1] + zin[which, 2]
        full6[cx, cy, cc, v] = piece

        def region(part, have, at):
            lo, n, _ = PARTS[part]
            ix, iy, iz = (
                pl.ds(0, 4) if d in have else pl.ds(at[d], 1) for d in "xyz")
            return full6.at[ix, iy, pl.ds(at["c"], 1), iz, :, pl.ds(lo, n)]

        me = dict(x=cx, y=cy, z=v, c=cc)

        def peer(d, k):
            at = dict(me)
            at[d] = (me[d] + k) % 4
            return at

        def device(at):
            return (at["z"], at["x"] * 8 + at["y"] * 2 + at["c"])

        def ag(part, phase, k):
            order = PARTS[part][2]
            have = order[:phase]
            return pltpu.make_async_remote_copy(
                src_ref=region(part, have, me), dst_ref=region(part, have, me),
                send_sem=ag_s.at[which], recv_sem=ag_r.at[which, part, phase],
                device_id=device(peer(order[phase], k)), device_id_type=MESH)

        def core(part, have, at):
            return pltpu.make_async_remote_copy(
                src_ref=region(part, have, at), dst_ref=region(part, have, at),
                send_sem=co_s.at[which], recv_sem=co_r.at[which],
                device_id=device(dict(me, c=1 - cc)), device_id_type=MESH)

        def ag_taken(part, phase):
            lo, n, _ = PARTS[part]
            taken(full.at[pl.ds(0, 24 * 4 ** phase), pl.ds(lo, n)], ag_r.at[which, part, phase])

        for phase in range(4):
            for part in range(3):
                order = PARTS[part][2]
                if phase:
                    ag_taken(part, phase - 1)
                    for k in (1, 3, 2):
                        core(part, order[:phase - 1], peer(order[phase - 1], k)).start()
                if phase < 3:
                    for k in (2, 1, 3):
                        ag(part, phase, k).start()
                if phase == 0:
                    core(part, "", me).start()
            if phase < 3:
                filler(phase)
        half_rows = full.at[pl.ds(0, N // 2), :]
        taken(half_rows, co_r.at[which])
        taken(half_rows, co_s.at[which])
        taken(zin.at[which], zs_s.at[which])
        taken(full.at[pl.ds(0, N // 2 - 8), :], ag_s.at[which])

    def nothing(phase):
        pass

    xh, xl = l1th, l1tl

    def prepare(phase):
        if phase == 0:
            @pl.loop(0, VECS // 4)
            def _(i):
                h, l = split(xf[pl.ds(i * 4, 4)].reshape(128, N))
                rows = pl.ds(pl.multiple_of(i * 128, 128), 128)
                xh[rows, :] = h
                xl[rows, :] = l

    with jax.named_scope("ex1"):
        exchange(full1, 0, prepare)

    def antisymmetric(full, high, low):
        def body(i, acc):
            at = pl.multiple_of(i * 128, 128)
            strip = full[pl.ds(at, 128), :] - full[:, pl.ds(at, 128)].T
            gf[pl.ds(at, 128), :] = strip
            h, l = split(strip)
            high[pl.ds(at, 128), :] = h
            low[pl.ds(at, 128), :] = l
            square = strip * strip
            return acc + jnp.sum(square.reshape(16, 8, N), axis=0)
        acc = lax.fori_loop(0, N // 128, body, jnp.zeros((8, N), F32))
        total = jnp.sum(jnp.sum(acc, axis=1, keepdims=True), axis=0, keepdims=True)
        norm = jnp.sqrt(total / (N * N) + 1e-06)
        return (STEP_GAIN / (N ** 0.5)) / norm

    def eye(i, j, m, n):
        rows = lax.broadcasted_iota(jnp.int32, (m, n), 0) + i
        cols = lax.broadcasted_iota(jnp.int32, (m, n), 1) + j
        return (rows == cols).astype(F32)

    with jax.named_scope("gen1"):
        scale = antisymmetric(full1, ah, al)

    def panels(body):
        @pl.loop(0, N // 256)
        def _(t):
            body(pl.ds(pl.multiple_of(t * 256, 256), 256), t * 256)

    def series(c, high, low):
        def store(rows, cols, i, j, sq):
            value = c * gf[rows, cols] + (0.5 * c * c) * sq
            h, l = split(value + eye(i, j, sq.shape[0], 256) if i <= j else value)
            high[rows, cols] = h
            low[rows, cols] = l

        for t in range(4):
            m, cols = 256 * (t + 1), pl.ds(256 * t, 256)
            sq = dot3(ah[pl.ds(0, m), :], al[pl.ds(0, m), :], ah[:, cols], al[:, cols])
            store(pl.ds(0, m), cols, 0, 256 * t, sq)
            for u in range(t):
                store(cols, pl.ds(256 * u, 256), 256 * t, 256 * u, sq[256 * u:256 * (u + 1), :].T)

    with jax.named_scope("step1"):
        series(scale, s1h, s1l)

    def left(cols, j):
        l1[:, :, cols] = dot3(xh[...], xl[...], s1h[:, cols], s1l[:, cols]).reshape(VECS, ROWS, 256)

    with jax.named_scope("left"):
        panels(left)

    mine = pl.ds(pl.multiple_of(r * ROWS, ROWS), ROWS)
    for t in range(8):
        cols = pl.ds(t * 128, 128)
        weight = s1h[mine, cols].astype(F32) + s1l[mine, cols].astype(F32)

        @pl.loop(0, VECS, unroll=8)
        def _(p):
            dpart[p, pl.ds(t, 1), :] = jnp.sum(l1[p, :, cols] * weight, axis=0, keepdims=True)

    def dsend(k):
        to = (r + k) % NR
        return pltpu.make_async_remote_copy(
            src_ref=dpart.at[to], dst_ref=din.at[k], send_sem=d_sem.at[0], recv_sem=d_sem.at[1],
            device_id=(v, to), device_id_type=MESH)

    def dback(k):
        to = (r + k) % NR
        return pltpu.make_async_remote_copy(
            src_ref=din.at[0], dst_ref=dfull.at[r], send_sem=d_sem.at[2], recv_sem=d_sem.at[3],
            device_id=(v, to), device_id_type=MESH)

    def others(sem):
        pltpu.make_async_copy(din.at[pl.ds(1, NR - 1)], din.at[pl.ds(1, NR - 1)], d_sem.at[sem]).wait()

    @pl.loop(1, NR)
    def _(k):
        dsend(k).start()

    with jax.named_scope("drecv"):
        others(1)

    total = dpart[r] + jnp.sum(din[pl.ds(1, NR - 1)], axis=0)
    din[0] = total
    dfull[r] = total

    @pl.loop(1, NR)
    def _(k):
        dback(k).start()

    def transposed(i):
        at = pl.multiple_of(i * 128, 128)
        strip = l1[pl.ds(i * 4, 4), :, :].reshape(128, N).T
        h, l = split(strip)
        l1th[:, pl.ds(at, 128)] = h
        l1tl[:, pl.ds(at, 128)] = l

    @pl.loop(0, N // 128)
    def _(i):
        transposed(i)

    with jax.named_scope("dback"):
        others(3)
    others(0)
    others(2)

    for t in range(8):
        cols = pl.ds(t * 128, 128)
        def body(p, acc):
            return acc + l1[p, :, cols] * dfull[p, pl.ds(t, 1), :]
        acc = lax.fori_loop(0, VECS, body, jnp.zeros((ROWS, 128), F32), unroll=4)
        own[:, :, cols] = acc.reshape(NV, 8, 128)

    with jax.named_scope("ex2"):
        exchange(full2, 1, nothing)

    @pl.loop(0, N // 128)
    def _(i):
        at = pl.multiple_of(i * 128, 128)
        h, l = split(full2[pl.ds(at, 128), :].T)
        ah[:, pl.ds(at, 128)] = h
        al[:, pl.ds(at, 128)] = l

    def own2(cols, j):
        stage[:, cols] = dot3(ah[...], al[...], s1h[:, cols], s1l[:, cols])

    with jax.named_scope("own2"):
        panels(own2)
    with jax.named_scope("gen2"):
        scale2 = antisymmetric(stage, ah, al)

    def partner(i, way):
        dx, dy, dc = OFFSETS[i]
        return ((cx + way * dx + 4) % 4) * 8 + ((cy + way * dy + 4) % 4) * 2 + (cc + dc) % 2

    def rows_of(device):
        return pl.ds(pl.multiple_of(device * ROWS, ROWS), ROWS)

    def big(g, i):
        to = partner(i, 1)
        lanes = pl.ds(pl.multiple_of(g * GW, GW), GW)
        return pltpu.make_async_remote_copy(
            src_ref=stage.at[rows_of(to), lanes], dst_ref=zbuf.at[mine, lanes],
            send_sem=big_s, recv_sem=big_r.at[g, OFFSETS[i][0]],
            device_id=(v, to), device_id_type=MESH)

    def big_taken(g, dx):
        ref = zbuf.at[pl.ds(0, (8 if dx else 7) * ROWS), pl.ds(g * GW, GW)]
        pltpu.make_async_copy(ref, ref, big_r.at[g, dx]).wait()

    @pl.loop(0, GROUPS)
    def _(g):
        lanes = pl.ds(pl.multiple_of(g * GW, GW), GW)
        with jax.named_scope("l2"):
            h, l = split(scale2 * dot3(ah[...], al[...], l1th[:, lanes], l1tl[:, lanes]))
            wh[...] = h
            wl[...] = l
            second = (0.5 * scale2) * dot3(ah[...], al[...], wh[...], wl[...])
            first = wh[...].astype(F32) + wl[...].astype(F32)
            stage[:, lanes] = (l1th[:, lanes].astype(F32) + l1tl[:, lanes].astype(F32)) + (second - first)
        for i in range(NR - 1):
            big(g, i).start()
        zbuf[mine, lanes] = stage[mine, lanes]

    def rotation(cols, j):
        h, l = split(dot3(s1h[...], s1l[...], s2h[:, cols], s2l[:, cols]))
        rh[:, cols] = h
        rl[:, cols] = l

    with jax.named_scope("step2"):
        series(scale2, s2h, s2l)
    with jax.named_scope("rot"):
        panels(rotation)
    rot_ref[...] = rh[mine, :].astype(F32) + rl[mine, :].astype(F32)

    group = lax.broadcasted_iota(jnp.int32, (ROWS, 128), 1) // ROWS

    def gathered(at, q, row, col):
        blocks = [
            zbuf[pl.ds(pl.multiple_of(at + b * ROWS, ROWS), ROWS), pl.ds(pl.multiple_of(q * 128, 128), 128)]
            for b in range(4)]
        for p in range(4):
            out = blocks[p]
            for b in range(4):
                if b != p:
                    turned = pltpu.roll(blocks[b], (ROWS * (b - p)) % 128, 1)
                    out = jnp.where(group == b, turned, out)
            h, l = split(out)
            rows = pl.ds(row + p * ROWS, ROWS)
            lh[rows, col] = h
            ll[rows, col] = l

    def finish(first, chunks):
        m = chunks * GW
        with jax.named_scope(f"bigwait{first}"):
            for g in range(first, first + chunks):
                for dx in range(4):
                    big_taken(g, dx)

        with jax.named_scope(f"turn{first}"):
            @pl.loop(0, 8)
            def _(b4):
                at = pl.multiple_of(b4 * 128, 128)
                for q in range(m // 128):
                    gathered(at, first * GW // 128 + q, q * 128, pl.ds(at, 128))

        with jax.named_scope(f"final{first}"):
            @pl.loop(0, 2)
            def _(j):
                cols = pl.ds(pl.multiple_of(j * 512, 512), 512)
                res = dot3(lh[pl.ds(0, m), :], ll[pl.ds(0, m), :], rh[:, cols], rl[:, cols])
                out_ref[pl.ds(first * GP, chunks * GP), :, cols] = res.reshape(chunks * GP, ROWS, 512)

    finish(0, 2)
    finish(2, 1)

    last = GROUPS - 1
    for dx in (2, 1, 3, 0):
        with jax.named_scope(f"bigwait3_{dx}"):
            big_taken(last, dx)
        at = pl.multiple_of(((cx + 4 - dx) % 4) * 256, 256)
        for b4 in range(2):
            for q in range(GW // 128):
                gathered(at + b4 * 128, last * GW // 128 + q, q * 128, pl.ds(b4 * 128, 128))

        @pl.loop(0, 2)
        def _(j):
            cols = pl.ds(pl.multiple_of(j * 512, 512), 512)
            depth, first = pl.ds(at, 256), pl.ds(0, GW)
            res = dot3(lh[first, pl.ds(0, 256)], ll[first, pl.ds(0, 256)], rh[depth, cols], rl[depth, cols])
            res = res.reshape(GP, ROWS, 512)
            if dx == 2:
                out_ref[pl.ds(last * GP, GP), :, cols] = res
            else:
                out_ref[pl.ds(last * GP, GP), :, cols] += res

    sent = stage.at[pl.ds(0, N - ROWS), :]
    pltpu.make_async_copy(sent, sent, big_s).wait()


def shards(chol_vectors):
    full = pltpu.VMEM((N, N), F32)
    half = pltpu.VMEM((N, N), BF16)
    sem = pltpu.SemaphoreType.DMA
    return pl.pallas_call(
        kernel,
        out_shape=(
            pltpu.VMEM((VECS, ROWS, N), F32),
            jax.ShapeDtypeStruct((ROWS, N), F32),
        ),
        in_specs=[pl.BlockSpec(memory_space=pl.ANY)],
        out_specs=(pl.BlockSpec(memory_space=pltpu.VMEM), pl.BlockSpec(memory_space=pltpu.VMEM)),
        scratch_shapes=[
            pltpu.VMEM((VECS, ROWS, N), F32),
            pltpu.VMEM((VECS, ROWS, 128), F32),
            pltpu.VMEM((NV, 8, N), F32),
            pltpu.VMEM((2, NV - 1, 8, N), F32),
            full,
            full,
            full,
            half, half, half, half,
            pltpu.VMEM((VECS, ROWS, N), F32),
            half, half,
            pltpu.VMEM((VECS, 8, 128), F32),
            pltpu.VMEM((NR, 8, 128), F32),
            pltpu.VMEM((NR, 8, 128), F32),
            full,
            half, half,
            full,
            half, half,
            pltpu.VMEM((N, GW), BF16), pltpu.VMEM((N, GW), BF16),
            pltpu.VMEM((2 * GW, N), BF16), pltpu.VMEM((2 * GW, N), BF16),
            sem,
            sem((2,)), sem((2,)),
            sem((2,)), sem((2, 3, 3)),
            sem((2,)), sem((2,)),
            sem((4,)),
            sem, sem((GROUPS, 4)),
        ],
        compiler_params=pltpu.CompilerParams(
            collective_id=0, has_side_effects=True, vmem_limit_bytes=VMEM_LIMIT
        ),
    )(chol_vectors)


def solution(mesh):
    return jax.shard_map(
        shards,
        mesh=mesh,
        in_specs=(P("vec", "row", None),),
        out_specs=(P("vec", "row", None), P("row", None)),
        check_vma=False,
    )
```

time: 193 us -> 159 us (0.82)
  Pallas kernels: 184 us -> 153 us
  local copies, waits for them, and re-layouts: 5.48 us -> 2.68 us
    pallas_call x1, Pallas kernels: 184 us -> 153 us  [shards(): pl.pallas_call(kernel, out_shape=(pltpu.VMEM((VECS, ROWS, N), F32), jax.S...]
    unnamed x4, local copies, waits for them, and re-layouts: 5.48 us -> 2.68 us
where the time goes in v2:
time: 159 us; the launch traced here: 156 us
  Pallas kernels  153 us (96%)
  local copies, waits for them, and re-layouts  2.68 us (2%)
    pallas_call x1, Pallas kernels, shards(): pl.pallas_call(kernel, out_shape=(pltpu.VMEM((VECS, ROWS, N), F32), jax.S...  153 us

profile of v2, /device:TPU:1, one launch (start us, length us, event | category | flops | bytes accessed | tf_op | source)
XLA Modules:
  0.0 156.5 jit_solution(2538331477206658644)
XLA Ops:
  0.6 153.1 %shard_map.30 = (f32[32,32,1024]{2,1,0:T(8,128)S(1)}, f32[32,1024]{1,0:T(8,128)}) custom-call(f32[32,32,1024]{2,1,0:T(8,128)} %x_ref.1), custom_call_target="tpu_custom_call" | custom-call | tf_op jit(solution)/shard_map/pallas_call | solution.py:423
  153.8 0.0 copy-start
  153.8 2.0 %copy.5 = f32[32,32,1024]{2,1,0:T(8,128)} copy(f32[32,32,1024]{2,1,0:T(8,128)S(1)} %get-tuple-element.2) | data formatting | bytes 8388608
  155.8 0.0 copy-done
  155.8 0.7 copy.6
Async XLA Ops:
  153.8 2.0 %copy-start = (f32[32,1024]{1,0:T(8,128)S(1)}, f32[32,1024]{1,0:T(8,128)}, u32[]{:S(2)}) copy-start(f32[32,1024]{1,0:T(8,128)} %get-tuple-element.7) | copy-start | bytes 393220

commit v3 on v2

--- a/solution.py
+++ b/solution.py
@@ -39,7 +39,7 @@
 def kernel(
     x_ref, out_ref, rot_ref,
     xf, dbuf, own, zin, full1, full2, gf, s1h, s1l, s2h, s2l,
-    l1, l1th, l1tl, dpart, din, dfull, zbuf, ah, al, stage, rh, rl, wh, wl, lh, ll,
+    l1, l1th, l1tl, dpart, din, dfull, zbuf, ah, al, stage, rh, rl, wh, wl, lh, ll, mh, ml,
     x_sem, zs_s, zs_r, ag_s, ag_r, co_s, co_r, d_sem, big_s, big_r,
 ):
     v = lax.axis_index("vec")
@@ -85,7 +85,7 @@
     weighted(lambda p, t: xf[p, :, pl.ds(t, 256)], lambda p, t: wide(dbuf[p]))
     pl.semaphore_wait(barrier, NR - 1 + NV - 1)
 
-    def exchange(full, which, filler):
+    def exchange(full, which, filler, consume=None):
         full6 = full.reshape(4, 4, 2, 4, 8, N)
 
         def zcopy(k):
@@ -126,36 +126,58 @@
             have = order[:phase]
             return pltpu.make_async_remote_copy(
                 src_ref=region(part, have, me), dst_ref=region(part, have, me),
-                send_sem=ag_s.at[which], recv_sem=ag_r.at[which, part, phase],
+                send_sem=ag_s.at[which], recv_sem=ag_r.at[which, part, phase + (k - 1 if phase == 2 else 0)],
                 device_id=device(peer(order[phase], k)), device_id_type=MESH)
 
-        def core(part, have, at):
+        def core(part, have, at, group):
             return pltpu.make_async_remote_copy(
                 src_ref=region(part, have, at), dst_ref=region(part, have, at),
-                send_sem=co_s.at[which], recv_sem=co_r.at[which],
+                send_sem=co_s.at[which], recv_sem=co_r.at[which, part, group],
                 device_id=device(dict(me, c=1 - cc)), device_id_type=MESH)
 
-        def ag_taken(part, phase):
+        def lanes_taken(part, rows, sem):
             lo, n, _ = PARTS[part]
-            taken(full.at[pl.ds(0, 24 * 4 ** phase), pl.ds(lo, n)], ag_r.at[which, part, phase])
-
-        for phase in range(4):
+            taken(full.at[pl.ds(0, rows), pl.ds(lo, n)], sem)
+
+        for phase in range(3):
             for part in range(3):
                 order = PARTS[part][2]
                 if phase:
-                    ag_taken(part, phase - 1)
+                    lanes_taken(part, 24 * 4 ** (phase - 1), ag_r.at[which, part, phase - 1])
                     for k in (1, 3, 2):
-                        core(part, order[:phase - 1], peer(order[phase - 1], k)).start()
-                if phase < 3:
-                    for k in (2, 1, 3):
-                        ag(part, phase, k).start()
+                        core(part, order[:phase - 1], peer(order[phase - 1], k), 0).start()
+                for k in ((1, 3, 2) if phase == 2 else (2, 1, 3)):
+                    ag(part, phase, k).start()
                 if phase == 0:
-                    core(part, "", me).start()
-            if phase < 3:
-                filler(phase)
-        half_rows = full.at[pl.ds(0, N // 2), :]
-        taken(half_rows, co_r.at[which])
-        taken(half_rows, co_s.at[which])
+                    core(part, "", me, 0).start()
+            filler(phase)
+
+        def arrived(k):
+            for part in range(3):
+                order = PARTS[part][2]
+                lanes_taken(part, 128, ag_r.at[which, part, 2 + k - 1])
+                core(part, order[:2], peer(order[2], 4 - k), k).start()
+
+        def use(k):
+            for part in range(3):
+                lanes_taken(part, 128, co_r.at[which, part, k])
+                if consume is not None:
+                    consume(part, peer(PARTS[part][2][2], (4 - k) % 4)[PARTS[part][2][2]], k == 0)
+
+        with jax.named_scope(f"use{which}_0"):
+            use(0)
+        with jax.named_scope(f"arr{which}_13"):
+            arrived(1)
+            arrived(3)
+        with jax.named_scope(f"use{which}_1"):
+            use(1)
+        with jax.named_scope(f"arr{which}_2"):
+            arrived(2)
+        with jax.named_scope(f"use{which}_3"):
+            use(3)
+        with jax.named_scope(f"use{which}_2"):
+            use(2)
+        taken(full.at[pl.ds(0, N // 2), :], co_s.at[which])
         taken(zin.at[which], zs_s.at[which])
         taken(full.at[pl.ds(0, N // 2 - 8), :], ag_s.at[which])
 
@@ -255,6 +277,17 @@
     def _(k):
         dsend(k).start()
 
+    for source, by_y, by_z in ((s1h, s2h, rh), (s1l, s2l, rl)):
+        @pl.loop(0, 16)
+        def _(b):
+            block = source[pl.ds(pl.multiple_of(b * 64, 64), 64), :]
+            by_y[pl.ds(pl.multiple_of((b % 4) * 256 + (b // 4) * 64, 64), 64), :] = block
+            wide_block = block.astype(F32)
+            for z in range(4):
+                pair = jnp.concatenate(
+                    [wide_block[8 * z:8 * z + 8, :], wide_block[32 + 8 * z:40 + 8 * z, :]], axis=0)
+                by_z[pl.ds(pl.multiple_of(z * 256 + b * 16, 16), 16), :] = pair.astype(BF16)
+
     with jax.named_scope("drecv"):
         others(1)
 
@@ -289,21 +322,34 @@
         acc = lax.fori_loop(0, VECS, body, jnp.zeros((ROWS, 128), F32), unroll=4)
         own[:, :, cols] = acc.reshape(NV, 8, 128)
 
+    full6 = full2.reshape(4, 4, 2, 4, 8, N)
+
+    def own2(part, at, first):
+        lo, n, order = PARTS[part]
+        lanes = pl.ds(lo, n)
+        rows = {
+            "x": lambda: full6[at, :, :, :, :, lanes],
+            "y": lambda: full6[:, at, :, :, :, lanes],
+            "z": lambda: full6[:, :, :, at, :, lanes],
+        }[order[2]]().reshape(256, n)
+        sh, sl = {"x": (s1h, s1l), "y": (s2h, s2l), "z": (rh, rl)}[order[2]]
+        h, l = split(rows.T)
+        mh[pl.ds(0, n), :] = h
+        ml[pl.ds(0, n), :] = l
+        depth = pl.ds(pl.multiple_of(at * 256, 256), 256)
+
+        @pl.loop(0, 2)
+        def _(j):
+            cols = pl.ds(pl.multiple_of(j * 512, 512), 512)
+            res = dot3(mh[pl.ds(0, n), :], ml[pl.ds(0, n), :], sh[depth, cols], sl[depth, cols])
+            if first:
+                stage[lanes, cols] = res
+            else:
+                stage[lanes, cols] += res
+
     with jax.named_scope("ex2"):
-        exchange(full2, 1, nothing)
-
-    @pl.loop(0, N // 128)
-    def _(i):
-        at = pl.multiple_of(i * 128, 128)
-        h, l = split(full2[pl.ds(at, 128), :].T)
-        ah[:, pl.ds(at, 128)] = h
-        al[:, pl.ds(at, 128)] = l
-
-    def own2(cols, j):
-        stage[:, cols] = dot3(ah[...], al[...], s1h[:, cols], s1l[:, cols])
-
-    with jax.named_scope("own2"):
-        panels(own2)
+        exchange(full2, 1, nothing, own2)
+
     with jax.named_scope("gen2"):
         scale2 = antisymmetric(stage, ah, al)
 
@@ -333,9 +379,14 @@
             h, l = split(scale2 * dot3(ah[...], al[...], l1th[:, lanes], l1tl[:, lanes]))
             wh[...] = h
             wl[...] = l
-            second = (0.5 * scale2) * dot3(ah[...], al[...], wh[...], wl[...])
-            first = wh[...].astype(F32) + wl[...].astype(F32)
-            stage[:, lanes] = (l1th[:, lanes].astype(F32) + l1tl[:, lanes].astype(F32)) + (second - first)
+            stage[:, lanes] = dot3(ah[...], al[...], wh[...], wl[...])
+
+            @pl.loop(0, 8)
+            def _(i):
+                rows = pl.ds(pl.multiple_of(i * 128, 128), 128)
+                base = l1th[rows, lanes].astype(F32) + l1tl[rows, lanes].astype(F32)
+                first = wh[rows, :].astype(F32) + wl[rows, :].astype(F32)
+                stage[rows, lanes] = base + ((0.5 * scale2) * stage[rows, lanes] - first)
         for i in range(NR - 1):
             big(g, i).start()
         zbuf[mine, lanes] = stage[mine, lanes]
@@ -393,7 +444,7 @@
     finish(2, 1)
 
     last = GROUPS - 1
-    for dx in (2, 1, 3, 0):
+    for dx in (1, 3, 0, 2):
         with jax.named_scope(f"bigwait3_{dx}"):
             big_taken(last, dx)
         at = pl.multiple_of(((cx + 4 - dx) % 4) * 256, 256)
@@ -407,7 +458,7 @@
             depth, first = pl.ds(at, 256), pl.ds(0, GW)
             res = dot3(lh[first, pl.ds(0, 256)], ll[first, pl.ds(0, 256)], rh[depth, cols], rl[depth, cols])
             res = res.reshape(GP, ROWS, 512)
-            if dx == 2:
+            if dx == 1:
                 out_ref[pl.ds(last * GP, GP), :, cols] = res
             else:
                 out_ref[pl.ds(last * GP, GP), :, cols] += res
@@ -424,7 +475,7 @@
         kernel,
         out_shape=(
             pltpu.VMEM((VECS, ROWS, N), F32),
-            jax.ShapeDtypeStruct((ROWS, N), F32),
+            pltpu.VMEM((ROWS, N), F32),
         ),
         in_specs=[pl.BlockSpec(memory_space=pl.ANY)],
         out_specs=(pl.BlockSpec(memory_space=pltpu.VMEM), pl.BlockSpec(memory_space=pltpu.VMEM)),
@@ -448,10 +499,11 @@
             half, half,
             pltpu.VMEM((N, GW), BF16), pltpu.VMEM((N, GW), BF16),
             pltpu.VMEM((2 * GW, N), BF16), pltpu.VMEM((2 * GW, N), BF16),
+            pltpu.VMEM((384, 256), BF16), pltpu.VMEM((384, 256), BF16),
             sem,
             sem((2,)), sem((2,)),
-            sem((2,)), sem((2, 3, 3)),
-            sem((2,)), sem((2,)),
+            sem((2,)), sem((2, 3, 5)),
+            sem((2,)), sem((2, 3, 4)),
             sem((4,)),
             sem, sem((GROUPS, 4)),
         ],

time: 159 us -> 154 us (0.969)
  Pallas kernels: 153 us -> 148 us
    pallas_call x1, Pallas kernels: 153 us -> 148 us  [shards(): pl.pallas_call(kernel, out_shape=(pltpu.VMEM((VECS, ROWS, N), F32), pltpu...]
where the time goes in v3:
time: 154 us; the launch traced here: 151 us
  Pallas kernels  148 us (96%)
  local copies, waits for them, and re-layouts  2.67 us (2%)
    pallas_call x1, Pallas kernels, shards(): pl.pallas_call(kernel, out_shape=(pltpu.VMEM((VECS, ROWS, N), F32), pltpu...  148 us

profile of v3, /device:TPU:1, one launch (start us, length us, event | category | flops | bytes accessed | tf_op | source)
XLA Modules:
  0.0 151.2 jit_solution(16905380534289272491)
XLA Ops:
  0.6 147.9 %shard_map.30 = (f32[32,32,1024]{2,1,0:T(8,128)S(1)}, f32[32,1024]{1,0:T(8,128)S(1)}) custom-call(f32[32,32,1024]{2,1,0:T(8,128)} %x_ref.1), custom_call_target="tpu_custom_call" | custom-call | tf_op jit(solution)/shard_map/pallas_call | solution.py:474
  148.6 2.0 %copy.5 = f32[32,32,1024]{2,1,0:T(8,128)} copy(f32[32,32,1024]{2,1,0:T(8,128)S(1)} %get-tuple-element.2) | data formatting | bytes 8388608
  150.6 0.7 copy.6

commit v4 on v3

--- a/solution.py
+++ b/solution.py
@@ -12,9 +12,9 @@
 NR = 32
 VECS = 32
 ROWS = 32
-GROUPS = 4
-GW = N // GROUPS
-GP = VECS // GROUPS
+GW = 256
+CW = 128
+CHUNKS = N // CW
 STEP_GAIN = 0.2
 VMEM_LIMIT = 58 << 20
 PARTS = ((0, 384, "zyx"), (384, 384, "xzy"), (768, 256, "yxz"))
@@ -208,7 +208,7 @@
             low[pl.ds(at, 128), :] = l
             square = strip * strip
             return acc + jnp.sum(square.reshape(16, 8, N), axis=0)
-        acc = lax.fori_loop(0, N // 128, body, jnp.zeros((8, N), F32))
+        acc = lax.fori_loop(0, N // 128, body, jnp.zeros((8, N), F32), unroll=2)
         total = jnp.sum(jnp.sum(acc, axis=1, keepdims=True), axis=0, keepdims=True)
         norm = jnp.sqrt(total / (N * N) + 1e-06)
         return (STEP_GAIN / (N ** 0.5)) / norm
@@ -254,7 +254,7 @@
         cols = pl.ds(t * 128, 128)
         weight = s1h[mine, cols].astype(F32) + s1l[mine, cols].astype(F32)
 
-        @pl.loop(0, VECS, unroll=8)
+        @pl.loop(0, VECS, unroll=16)
         def _(p):
             dpart[p, pl.ds(t, 1), :] = jnp.sum(l1[p, :, cols] * weight, axis=0, keepdims=True)
 
@@ -338,14 +338,11 @@
         ml[pl.ds(0, n), :] = l
         depth = pl.ds(pl.multiple_of(at * 256, 256), 256)
 
-        @pl.loop(0, 2)
-        def _(j):
-            cols = pl.ds(pl.multiple_of(j * 512, 512), 512)
-            res = dot3(mh[pl.ds(0, n), :], ml[pl.ds(0, n), :], sh[depth, cols], sl[depth, cols])
-            if first:
-                stage[lanes, cols] = res
-            else:
-                stage[lanes, cols] += res
+        res = dot3(mh[pl.ds(0, n), :], ml[pl.ds(0, n), :], sh[depth, :], sl[depth, :])
+        if first:
+            stage[lanes, :] = res
+        else:
+            stage[lanes, :] += res
 
     with jax.named_scope("ex2"):
         exchange(full2, 1, nothing, own2)
@@ -362,24 +359,24 @@
 
     def big(g, i):
         to = partner(i, 1)
-        lanes = pl.ds(pl.multiple_of(g * GW, GW), GW)
+        lanes = pl.ds(pl.multiple_of(g * CW, CW), CW)
         return pltpu.make_async_remote_copy(
             src_ref=stage.at[rows_of(to), lanes], dst_ref=zbuf.at[mine, lanes],
-            send_sem=big_s, recv_sem=big_r.at[g, OFFSETS[i][0]],
+            send_sem=big_s, recv_sem=big_r.at[g],
             device_id=(v, to), device_id_type=MESH)
 
-    def big_taken(g, dx):
-        ref = zbuf.at[pl.ds(0, (8 if dx else 7) * ROWS), pl.ds(g * GW, GW)]
-        pltpu.make_async_copy(ref, ref, big_r.at[g, dx]).wait()
-
-    @pl.loop(0, GROUPS)
+    @pl.loop(0, N // GW)
     def _(g):
         lanes = pl.ds(pl.multiple_of(g * GW, GW), GW)
         with jax.named_scope("l2"):
-            h, l = split(scale2 * dot3(ah[...], al[...], l1th[:, lanes], l1tl[:, lanes]))
-            wh[...] = h
-            wl[...] = l
-            stage[:, lanes] = dot3(ah[...], al[...], wh[...], wl[...])
+            for u in range(2):
+                rows = pl.ds(u * 512, 512)
+                h, l = split(scale2 * dot3(ah[rows, :], al[rows, :], l1th[:, lanes], l1tl[:, lanes]))
+                wh[rows, :] = h
+                wl[rows, :] = l
+            for u in range(2):
+                rows = pl.ds(u * 512, 512)
+                stage[rows, lanes] = dot3(ah[rows, :], al[rows, :], wh[...], wl[...])
 
             @pl.loop(0, 8)
             def _(i):
@@ -387,8 +384,10 @@
                 base = l1th[rows, lanes].astype(F32) + l1tl[rows, lanes].astype(F32)
                 first = wh[rows, :].astype(F32) + wl[rows, :].astype(F32)
                 stage[rows, lanes] = base + ((0.5 * scale2) * stage[rows, lanes] - first)
-        for i in range(NR - 1):
-            big(g, i).start()
+
+        for u in range(GW // CW):
+            for i in range(NR - 1):
+                big(g * (GW // CW) + u, i).start()
         zbuf[mine, lanes] = stage[mine, lanes]
 
     def rotation(cols, j):
@@ -419,49 +418,31 @@
             lh[rows, col] = h
             ll[rows, col] = l
 
-    def finish(first, chunks):
-        m = chunks * GW
+    def finish(first, chunks, width):
+        m = chunks * CW
         with jax.named_scope(f"bigwait{first}"):
             for g in range(first, first + chunks):
-                for dx in range(4):
-                    big_taken(g, dx)
+                ref = zbuf.at[pl.ds(0, N - ROWS), pl.ds(g * CW, CW)]
+                pltpu.make_async_copy(ref, ref, big_r.at[g]).wait()
 
         with jax.named_scope(f"turn{first}"):
-            @pl.loop(0, 8)
+            @pl.loop(0, 8, unroll=2 if chunks == 1 else None)
             def _(b4):
                 at = pl.multiple_of(b4 * 128, 128)
-                for q in range(m // 128):
-                    gathered(at, first * GW // 128 + q, q * 128, pl.ds(at, 128))
+                for q in range(chunks):
+                    gathered(at, first + q, q * 128, pl.ds(at, 128))
 
         with jax.named_scope(f"final{first}"):
-            @pl.loop(0, 2)
+            @pl.loop(0, N // width)
             def _(j):
-                cols = pl.ds(pl.multiple_of(j * 512, 512), 512)
+                cols = pl.ds(pl.multiple_of(j * width, width), width)
                 res = dot3(lh[pl.ds(0, m), :], ll[pl.ds(0, m), :], rh[:, cols], rl[:, cols])
-                out_ref[pl.ds(first * GP, chunks * GP), :, cols] = res.reshape(chunks * GP, ROWS, 512)
-
-    finish(0, 2)
-    finish(2, 1)
-
-    last = GROUPS - 1
-    for dx in (1, 3, 0, 2):
-        with jax.named_scope(f"bigwait3_{dx}"):
-            big_taken(last, dx)
-        at = pl.multiple_of(((cx + 4 - dx) % 4) * 256, 256)
-        for b4 in range(2):
-            for q in range(GW // 128):
-                gathered(at + b4 * 128, last * GW // 128 + q, q * 128, pl.ds(b4 * 128, 128))
-
-        @pl.loop(0, 2)
-        def _(j):
-            cols = pl.ds(pl.multiple_of(j * 512, 512), 512)
-            depth, first = pl.ds(at, 256), pl.ds(0, GW)
-            res = dot3(lh[first, pl.ds(0, 256)], ll[first, pl.ds(0, 256)], rh[depth, cols], rl[depth, cols])
-            res = res.reshape(GP, ROWS, 512)
-            if dx == 1:
-                out_ref[pl.ds(last * GP, GP), :, cols] = res
-            else:
-                out_ref[pl.ds(last * GP, GP), :, cols] += res
+                out_ref[pl.ds(first * 4, chunks * 4), :, cols] = res.reshape(chunks * 4, ROWS, width)
+
+    finish(0, 4, 512)
+    finish(4, 2, 512)
+    finish(6, 1, 1024)
+    finish(7, 1, 1024)
 
     sent = stage.at[pl.ds(0, N - ROWS), :]
     pltpu.make_async_copy(sent, sent, big_s).wait()
@@ -505,7 +486,7 @@
             sem((2,)), sem((2, 3, 5)),
             sem((2,)), sem((2, 3, 4)),
             sem((4,)),
-            sem, sem((GROUPS, 4)),
+            sem, sem((CHUNKS,)),
         ],
         compiler_params=pltpu.CompilerParams(
             collective_id=0, has_side_effects=True, vmem_limit_bytes=VMEM_LIMIT

time: 154 us -> 146 us (0.948)
  the two profiles are of different devices: /device:TPU:1 before, /device:TPU:39 now
where the time goes in v4:
time: 146 us
  Pallas kernels  143 us (98%)
  local copies, waits for them, and re-layouts  2.67 us (2%)
    pallas_call x1, Pallas kernels, shards(): pl.pallas_call(kernel, out_shape=(pltpu.VMEM((VECS, ROWS, N), F32), pltpu...  143 us

profile of v4, /device:TPU:39, one launch (start us, length us, event | category | flops | bytes accessed | tf_op | source)
XLA Modules:
  0.0 146.3 jit_solution(44558836920884478)
XLA Ops:
  0.6 143.0 %shard_map.30 = (f32[32,32,1024]{2,1,0:T(8,128)S(1)}, f32[32,1024]{1,0:T(8,128)S(1)}) custom-call(f32[32,32,1024]{2,1,0:T(8,128)} %x_ref.1), custom_call_target="tpu_custom_call" | custom-call | tf_op jit(solution)/shard_map/pallas_call | solution.py:455
  143.6 2.0 %copy.5 = f32[32,32,1024]{2,1,0:T(8,128)} copy(f32[32,32,1024]{2,1,0:T(8,128)S(1)} %get-tuple-element.2) | data formatting | bytes 8388608
  145.7 0.7 copy.6

commit v5 on v4

--- a/solution.py
+++ b/solution.py
@@ -16,7 +16,7 @@
 CW = 128
 CHUNKS = N // CW
 STEP_GAIN = 0.2
-VMEM_LIMIT = 58 << 20
+VMEM_LIMIT = 54 << 20
 PARTS = ((0, 384, "zyx"), (384, 384, "xzy"), (768, 256, "yxz"))
 OFFSETS = tuple(sorted(
     ((dx, dy, dc) for dx in range(4) for dy in range(4) for dc in range(2) if dx or dy or dc),
@@ -36,36 +36,75 @@
     return dot(ah, bh) + dot(ah, bl) + dot(al, bh)
 
 
+def gathered(z, high, low, at, lane, row):
+    group = lax.broadcasted_iota(jnp.int32, (ROWS, 128), 1) // ROWS
+    blocks = [
+        z[pl.ds(pl.multiple_of(at + b * ROWS, ROWS), ROWS), pl.ds(pl.multiple_of(lane, 128), 128)]
+        for b in range(4)]
+    for p in range(4):
+        out = blocks[p]
+        for b in range(4):
+            if b != p:
+                turned = pltpu.roll(blocks[b], (ROWS * (b - p)) % 128, 1)
+                out = jnp.where(group == b, turned, out)
+        h, l = split(out)
+        rows = pl.ds(row + p * ROWS, ROWS)
+        high[rows, pl.ds(at, 128)] = h
+        low[rows, pl.ds(at, 128)] = l
+
+
+def tail(done_ref, rot_in, last_ref, rh, rl, out_ref, rot_ref, lh, ll, res, sems):
+    held = VECS - 4
+    copies = [
+        pltpu.make_async_copy(done_ref.at[pl.ds(g * 7, 7)], out_ref.at[pl.ds(g * 7, 7)], sems.at[g])
+        for g in range(held // 7)]
+    copies.append(pltpu.make_async_copy(rot_in, rot_ref, sems.at[4]))
+    for copy in copies:
+        copy.start()
+
+    @pl.loop(0, 8, unroll=2)
+    def _(b4):
+        gathered(last_ref, lh, ll, pl.multiple_of(b4 * 128, 128), 0, 0)
+
+    res[...] = dot3(lh[...], ll[...], rh[...], rl[...]).reshape(4, ROWS, N)
+    copies.append(pltpu.make_async_copy(res, out_ref.at[pl.ds(held, 4)], sems.at[5]))
+    copies[-1].start()
+    for copy in copies:
+        copy.wait()
+
+
 def kernel(
-    x_ref, out_ref, rot_ref,
+    x_ref, out_ref, rot_ref, last_ref, rh, rl,
     xf, dbuf, own, zin, full1, full2, gf, s1h, s1l, s2h, s2l,
-    l1, l1th, l1tl, dpart, din, dfull, zbuf, ah, al, stage, rh, rl, wh, wl, lh, ll, mh, ml,
+    l1, l1th, l1tl, dpart, din, dfull, zbuf, ah, al, stage, wh, wl, lh, ll, mh, ml,
     x_sem, zs_s, zs_r, ag_s, ag_r, co_s, co_r, d_sem, big_s, big_r,
 ):
     v = lax.axis_index("vec")
     r = lax.axis_index("row")
     cx, cy, cc = r // 8, (r // 2) % 4, r % 2
 
-    load = pltpu.make_async_copy(x_ref, xf, x_sem)
-    load.start()
+    loads = [
+        pltpu.make_async_copy(x_ref.at[pl.ds(g * 8, 8)], xf.at[pl.ds(g * 8, 8)], x_sem.at[g])
+        for g in range(VECS // 8)]
+    for load in loads:
+        load.start()
+
+    def partner(i, way):
+        dx, dy, dc = OFFSETS[i]
+        return ((cx + way * dx + 4) % 4) * 8 + ((cy + way * dy + 4) % 4) * 2 + (cc + dc) % 2
+
     barrier = pltpu.get_barrier_semaphore()
-
-    @pl.loop(1, NR)
-    def _(k):
-        pl.semaphore_signal(barrier, inc=1, device_id=(v, (r + k) % NR), device_id_type=MESH)
-
-    @pl.loop(1, NV)
-    def _(k):
+    for i in range(NR - 1):
+        pl.semaphore_signal(barrier, inc=1, device_id=(v, partner(i, 1)), device_id_type=MESH)
+    for k in range(1, NV):
         pl.semaphore_signal(barrier, inc=1, device_id=((v + k) % NV, r), device_id_type=MESH)
-
-    load.wait()
 
     window = pl.multiple_of((r // 4) * 128, 128)
     lane = lax.broadcasted_iota(jnp.int32, (8, ROWS, 128), 2)
     sub = lax.broadcasted_iota(jnp.int32, (8, ROWS, 128), 1)
 
-    @pl.loop(0, VECS // 8)
-    def _(g):
+    for g, load in enumerate(loads):
+        load.wait()
         block = xf[pl.ds(g * 8, 8), :, pl.ds(window, 128)]
         picked = jnp.where(lane == sub + (r % 4) * ROWS, block, 0.0)
         dbuf[pl.ds(g * 8, 8)] = jnp.broadcast_to(
@@ -258,14 +297,14 @@
         def _(p):
             dpart[p, pl.ds(t, 1), :] = jnp.sum(l1[p, :, cols] * weight, axis=0, keepdims=True)
 
-    def dsend(k):
-        to = (r + k) % NR
+    def dsend(i):
+        to = partner(i, 1)
         return pltpu.make_async_remote_copy(
-            src_ref=dpart.at[to], dst_ref=din.at[k], send_sem=d_sem.at[0], recv_sem=d_sem.at[1],
+            src_ref=dpart.at[to], dst_ref=din.at[i + 1], send_sem=d_sem.at[0], recv_sem=d_sem.at[1],
             device_id=(v, to), device_id_type=MESH)
 
-    def dback(k):
-        to = (r + k) % NR
+    def dback(i):
+        to = partner(i, 1)
         return pltpu.make_async_remote_copy(
             src_ref=din.at[0], dst_ref=dfull.at[r], send_sem=d_sem.at[2], recv_sem=d_sem.at[3],
             device_id=(v, to), device_id_type=MESH)
@@ -273,9 +312,8 @@
     def others(sem):
         pltpu.make_async_copy(din.at[pl.ds(1, NR - 1)], din.at[pl.ds(1, NR - 1)], d_sem.at[sem]).wait()
 
-    @pl.loop(1, NR)
-    def _(k):
-        dsend(k).start()
+    for i in range(NR - 1):
+        dsend(i).start()
 
     for source, by_y, by_z in ((s1h, s2h, rh), (s1l, s2l, rl)):
         @pl.loop(0, 16)
@@ -295,9 +333,8 @@
     din[0] = total
     dfull[r] = total
 
-    @pl.loop(1, NR)
-    def _(k):
-        dback(k).start()
+    for i in range(NR - 1):
+        dback(i).start()
 
     def transposed(i):
         at = pl.multiple_of(i * 128, 128)
@@ -350,10 +387,6 @@
     with jax.named_scope("gen2"):
         scale2 = antisymmetric(stage, ah, al)
 
-    def partner(i, way):
-        dx, dy, dc = OFFSETS[i]
-        return ((cx + way * dx + 4) % 4) * 8 + ((cy + way * dy + 4) % 4) * 2 + (cc + dc) % 2
-
     def rows_of(device):
         return pl.ds(pl.multiple_of(device * ROWS, ROWS), ROWS)
 
@@ -401,23 +434,6 @@
         panels(rotation)
     rot_ref[...] = rh[mine, :].astype(F32) + rl[mine, :].astype(F32)
 
-    group = lax.broadcasted_iota(jnp.int32, (ROWS, 128), 1) // ROWS
-
-    def gathered(at, q, row, col):
-        blocks = [
-            zbuf[pl.ds(pl.multiple_of(at + b * ROWS, ROWS), ROWS), pl.ds(pl.multiple_of(q * 128, 128), 128)]
-            for b in range(4)]
-        for p in range(4):
-            out = blocks[p]
-            for b in range(4):
-                if b != p:
-                    turned = pltpu.roll(blocks[b], (ROWS * (b - p)) % 128, 1)
-                    out = jnp.where(group == b, turned, out)
-            h, l = split(out)
-            rows = pl.ds(row + p * ROWS, ROWS)
-            lh[rows, col] = h
-            ll[rows, col] = l
-
     def finish(first, chunks, width):
         m = chunks * CW
         with jax.named_scope(f"bigwait{first}"):
@@ -430,7 +446,7 @@
             def _(b4):
                 at = pl.multiple_of(b4 * 128, 128)
                 for q in range(chunks):
-                    gathered(at, first + q, q * 128, pl.ds(at, 128))
+                    gathered(zbuf, lh, ll, at, (first + q) * 128, q * 128)
 
         with jax.named_scope(f"final{first}"):
             @pl.loop(0, N // width)
@@ -442,7 +458,9 @@
     finish(0, 4, 512)
     finish(4, 2, 512)
     finish(6, 1, 1024)
-    finish(7, 1, 1024)
+    ref = zbuf.at[pl.ds(0, N - ROWS), pl.ds(0, CW)]
+    pltpu.make_async_copy(ref, ref, big_r.at[CHUNKS - 1]).wait()
+    last_ref[...] = zbuf[:, pl.ds(N - CW, CW)]
 
     sent = stage.at[pl.ds(0, N - ROWS), :]
     pltpu.make_async_copy(sent, sent, big_s).wait()
@@ -452,14 +470,15 @@
     full = pltpu.VMEM((N, N), F32)
     half = pltpu.VMEM((N, N), BF16)
     sem = pltpu.SemaphoreType.DMA
-    return pl.pallas_call(
+    outs = pl.pallas_call(
         kernel,
         out_shape=(
             pltpu.VMEM((VECS, ROWS, N), F32),
             pltpu.VMEM((ROWS, N), F32),
+            pltpu.VMEM((N, CW), F32), half, half,
         ),
         in_specs=[pl.BlockSpec(memory_space=pl.ANY)],
-        out_specs=(pl.BlockSpec(memory_space=pltpu.VMEM), pl.BlockSpec(memory_space=pltpu.VMEM)),
+        out_specs=(pl.BlockSpec(memory_space=pltpu.VMEM),) * 5,
         scratch_shapes=[
             pltpu.VMEM((VECS, ROWS, N), F32),
             pltpu.VMEM((VECS, ROWS, 128), F32),
@@ -477,11 +496,10 @@
             full,
             half, half,
             full,
-            half, half,
             pltpu.VMEM((N, GW), BF16), pltpu.VMEM((N, GW), BF16),
             pltpu.VMEM((2 * GW, N), BF16), pltpu.VMEM((2 * GW, N), BF16),
             pltpu.VMEM((384, 256), BF16), pltpu.VMEM((384, 256), BF16),
-            sem,
+            sem((VECS // 8,)),
             sem((2,)), sem((2,)),
             sem((2,)), sem((2, 3, 5)),
             sem((2,)), sem((2, 3, 4)),
@@ -492,6 +510,20 @@
             collective_id=0, has_side_effects=True, vmem_limit_bytes=VMEM_LIMIT
         ),
     )(chol_vectors)
+    return pl.pallas_call(
+        tail,
+        out_shape=(
+            jax.ShapeDtypeStruct((VECS, ROWS, N), F32),
+            jax.ShapeDtypeStruct((ROWS, N), F32),
+        ),
+        in_specs=[pl.BlockSpec(memory_space=pltpu.VMEM)] * 5,
+        out_specs=(pl.BlockSpec(memory_space=pl.ANY), pl.BlockSpec(memory_space=pl.ANY)),
+        scratch_shapes=[
+            pltpu.VMEM((CW, N), BF16), pltpu.VMEM((CW, N), BF16),
+            pltpu.VMEM((4, ROWS, N), F32), sem((6,)),
+        ],
+        compiler_params=pltpu.CompilerParams(vmem_limit_bytes=8 << 20),
+    )(*outs)
 
 
 def solution(mesh):

time: 146 us -> 143 us (0.979)
  the two profiles are of different devices: /device:TPU:39 before, /device:TPU:1 now
where the time goes in v5:
time: 143 us; the launch traced here: 140 us
  Pallas kernels  139 us (97%)
    pallas_call x1, Pallas kernels, shards(): pl.pallas_call(kernel, out_shape=(pltpu.VMEM((VECS, ROWS, N), F32), pltpu...  137 us

profile of v5, /device:TPU:1, one launch (start us, length us, event | category | flops | bytes accessed | tf_op | source)
XLA Modules:
  0.0 140.0 jit_solution(6147768636062766684)
XLA Ops:
  0.6 136.6 %shard_map.30 = (f32[32,32,1024]{2,1,0:T(8,128)S(1)}, f32[32,1024]{1,0:T(8,128)S(1)}, f32[1024,128]{1,0:T(8,128)S(1)}, bf16[1024,1024]{1,0:T(8,128)(2,1)S(1)}, bf16[1024,1024]{1,0:T(8,128)(2,1)S(1)}) custom-call(f32[32,32,1024]{2,1,0:T(8,128)} %x_ref.1), custom_call_target="tpu_custom_call" | custom-call | tf_op jit(solution)/shard_map/pallas_call | solution.py:473
  137.3 2.5 %shard_map.31 = (f32[32,32,1024]{2,1,0:T(8,128)}, f32[32,1024]{1,0:T(8,128)}) custom-call(f32[32,32,1024]{2,1,0:T(8,128)S(1)} %get-tuple-element.7.done_ref, f32[32,1024]{1,0:T(8,128)S(1)} %get-tuple-element.8.rot_in, f32[1024,128]{1,0:T(8,128)S(1)} %get-tuple-element.9.last_ref, bf16[1024,1024]{1,0:T(8,128)(2,1)S(1)} %get-tuple-element.10.rh, ...), custom_call_target="tpu_custom_call" | custom-call | tf_op jit(solution)/shard_map/pallas_call | solution.py:513
